TPU v7x, 32 devices: a whole 2x2x4 slice. The times are simulated.
32 devices in a mesh: seq: 4 (over y, core), fsdp: 8 (over z, x).
Axes of the slice: x: 2, y: 2, z: 4, core: 2. Of those that a mesh axis runs over, the one named last changes fastest.
Arguments:
- tokens: bfloat16 [8, 1024, 2048], P('fsdp', 'seq'), may hold values from -6 to 6
- teacher: bfloat16 [8, 1024, 2048], P('fsdp', 'seq'), may hold values from -6 to 6
- segments: int32 [8, 1024], P('fsdp'), may hold values from 0 to 3, never falling along the last dimension, each value on 1 to 512 neighbouring positions
- valid: int32 [8, 1024], P('fsdp', 'seq'), may hold values from 0 to 1, as said below
- ln1_gain: bfloat16 [2048], P('fsdp'), may hold values from 0.099609375 to 1.8984375
- ln1_bias: bfloat16 [2048], P('fsdp'), may hold values from -1.75 to 1.75
- w_qkv: bfloat16 [2048, 6144], P('fsdp'), may hold values from -0.125 to 0.125
- b_qkv: bfloat16 [6144], P('fsdp'), may hold values from -1.75 to 1.75
- w_out: bfloat16 [2048, 2048], P('fsdp'), may hold values from -0.5 to 0.5
- ln2_gain: bfloat16 [2048], P('fsdp'), may hold values from 0.099609375 to 1.8984375
- ln2_bias: bfloat16 [2048], P('fsdp'), may hold values from -1.75 to 1.75
- w_gate_up: bfloat16 [5632, 2, 2048], P('fsdp'), may hold values from -0.125 to 0.125
- w_down: bfloat16 [5632, 2048], P('fsdp'), may hold values from -0.15625 to 0.15625
Outputs:
- layer_out: bfloat16 [8, 1024, 2048], P('fsdp', 'seq')
- loss: float32 [], replicated
- grad_tokens: bfloat16 [8, 1024, 2048], P('fsdp', 'seq')
- grad_ln1_gain: float32 [2048], P('fsdp')
- grad_ln1_bias: float32 [2048], P('fsdp')
- grad_w_qkv: float32 [2048, 6144], P('fsdp')
- grad_b_qkv: float32 [6144], P('fsdp')
- grad_w_out: float32 [2048, 2048], P('fsdp')
- grad_ln2_gain: float32 [2048], P('fsdp')
- grad_ln2_bias: float32 [2048], P('fsdp')
- grad_w_gate_up: float32 [5632, 2, 2048], P('fsdp')
- grad_w_down: float32 [5632, 2048], P('fsdp')
Inputs may be any that keep to these rules, and one draw needn't show every extreme that they name: `segments`: segment numbers start at 0 in each sequence and never fall; each document has 1 to 512 tokens and one document of each sequence has exactly that many. `valid`: the first token of every sequence counts.
All inputs are finite; a program needn't handle non-finite values.
Results may differ from a plain program's by a relative error of at most 0.01.
Values may be sent and summed in bfloat16 or wider, within the bound.
No kernel may reach another device: no remote copies, remote signals or barrier semaphores. Data moves between devices by JAX's collectives and lax.ppermute only.
A program may use at most 704 MiB of HBM per device.

v0:
```python
import jax
import jax.numpy as jnp
from jax import lax
from jax.sharding import PartitionSpec as P

H = 32
HD = 64
ROT = 16
EPSILON = 1e-05
MASKED_VALUE = -1e30


def norm_parts(values):
    mean_value = jnp.mean(values, axis=-1, keepdims=True)
    centered = values - mean_value
    variance = jnp.mean(centered * centered, axis=-1, keepdims=True)
    inv_std = lax.rsqrt(variance + EPSILON)
    return (centered * inv_std, inv_std)


def norm_back(grad_out, normed, inv_std, gain_vec):
    scaled = grad_out * gain_vec
    mean_scaled = jnp.mean(scaled, axis=-1, keepdims=True)
    mean_cross = jnp.mean(scaled * normed, axis=-1, keepdims=True)
    return inv_std * (scaled - mean_scaled - normed * mean_cross)


def doc_positions(segment):
    places = jnp.arange(segment.shape[0], dtype=jnp.int32)
    change = jnp.concatenate([jnp.ones((1,), dtype=bool), segment[1:] != segment[:-1]])
    starts = lax.cummax(jnp.where(change, places, 0), axis=0)
    return places - starts


def rotate(values, positions, turn_sign):
    half_rot = ROT // 2
    inverse = 10000.0 ** (-(jnp.arange(half_rot, dtype=jnp.float32) * 2.0) / ROT)
    angles = positions.astype(jnp.float32)[:, None] * inverse[None, :]
    cosine = jnp.cos(angles)[:, None, :]
    sine_part = turn_sign * jnp.sin(angles)[:, None, :]
    front_half = values[..., :half_rot]
    back_half = values[..., half_rot:ROT]
    return jnp.concatenate(
        [
            front_half * cosine - back_half * sine_part,
            back_half * cosine + front_half * sine_part,
            values[..., ROT:],
        ],
        axis=-1,
    )


def gate_backward(gate_up, hidden_grad):
    gate_part = gate_up[:, 0]
    up_part = gate_up[:, 1]
    gate_sig = jax.nn.sigmoid(gate_part)
    up_grad = hidden_grad * (gate_part * gate_sig)
    silu_grad = hidden_grad * up_part
    gate_grad = silu_grad * gate_sig + silu_grad * gate_part * gate_sig * (1.0 - gate_sig)
    return jnp.stack([gate_grad, up_grad], axis=1).astype(jnp.bfloat16)


def block_scores(query_block, key_rows, block_seg, segment, first_row, score_scale):
    block_size = query_block.shape[0]
    places = jnp.arange(segment.shape[0], dtype=jnp.int32)
    block_places = first_row + jnp.arange(block_size, dtype=jnp.int32)
    allowed = (block_seg[:, None] == segment[None, :]) & (block_places[:, None] >= places[None, :])
    scores = (
        jnp.einsum("bhd,lhd->hbl", query_block, key_rows, preferred_element_type=jnp.float32)
        * score_scale
    )
    return jnp.where(allowed[None], scores, MASKED_VALUE)


def attention_forward(query_rows, key_rows, value_rows, segment, block_size, score_scale):
    length_total = key_rows.shape[0]

    def one_block(unused, first_row):
        query_block = lax.dynamic_slice_in_dim(query_rows, first_row, block_size, 0)
        block_seg = lax.dynamic_slice_in_dim(segment, first_row, block_size, 0)
        scores = block_scores(query_block, key_rows, block_seg, segment, first_row, score_scale)
        row_max = jnp.max(scores, axis=-1, keepdims=True)
        exp_scores = jnp.exp(scores - row_max)
        row_sum = jnp.sum(exp_scores, axis=-1, keepdims=True)
        probs = (exp_scores / row_sum).astype(jnp.bfloat16)
        block_out = jnp.einsum(
            "hbl,lhd->bhd", probs, value_rows, preferred_element_type=jnp.float32
        )
        return (unused, (block_out.astype(jnp.bfloat16), (row_max + jnp.log(row_sum))[..., 0]))

    firsts = jnp.arange(length_total // block_size, dtype=jnp.int32) * block_size
    unused, (block_outs, log_totals) = lax.scan(one_block, jnp.zeros((), jnp.int32), firsts)
    return (block_outs.reshape(length_total, query_rows.shape[1], query_rows.shape[2]), log_totals)


def attention_backward(
    query_rows, key_rows, value_rows, out_grad, log_totals, segment, block_size, score_scale
):
    length_total = key_rows.shape[0]

    def one_block(grad_carry, block_inputs):
        key_grad, value_grad = grad_carry
        first_row, block_log = block_inputs
        query_block = lax.dynamic_slice_in_dim(query_rows, first_row, block_size, 0)
        grad_block = lax.dynamic_slice_in_dim(out_grad, first_row, block_size, 0)
        block_seg = lax.dynamic_slice_in_dim(segment, first_row, block_size, 0)
        scores = block_scores(query_block, key_rows, block_seg, segment, first_row, score_scale)
        probs = jnp.exp(scores - block_log[..., None])
        prob_low = probs.astype(jnp.bfloat16)
        value_grad = value_grad + jnp.einsum(
            "hbl,bhd->lhd", prob_low, grad_block, preferred_element_type=jnp.float32
        )
        prob_grad = jnp.einsum(
            "bhd,lhd->hbl", grad_block, value_rows, preferred_element_type=jnp.float32
        )
        row_dot = jnp.sum(probs * prob_grad, axis=-1, keepdims=True)
        score_grad = (probs * (prob_grad - row_dot)).astype(jnp.bfloat16)
        query_grad = (
            jnp.einsum("hbl,lhd->bhd", score_grad, key_rows, preferred_element_type=jnp.float32)
            * score_scale
        )
        key_grad = (
            key_grad
            + jnp.einsum(
                "hbl,bhd->lhd", score_grad, query_block, preferred_element_type=jnp.float32
            )
            * score_scale
        )
        return ((key_grad, value_grad), query_grad)

    firsts = jnp.arange(length_total // block_size, dtype=jnp.int32) * block_size
    zero_grad = jnp.zeros(key_rows.shape, jnp.float32)
    (key_grad, value_grad), query_grads = lax.scan(
        one_block, (zero_grad, zero_grad), (firsts, log_totals)
    )
    return (query_grads.reshape(key_rows.shape), key_grad, value_grad)


def reduce_rows(term_rows, row_share):
    return lax.psum_scatter(
        term_rows(jnp.int32(0), row_share * lax.axis_size("fsdp")).astype(jnp.bfloat16),
        "fsdp",
        scatter_dimension=0,
        tiled=True,
    ).astype(jnp.float32)


def per_device(
    tokens,
    teacher,
    segments,
    valid,
    ln1_gain,
    ln1_bias,
    w_qkv,
    b_qkv,
    w_out,
    ln2_gain,
    ln2_bias,
    w_gate_up,
    w_down,
):
    seq_count = lax.axis_size("seq")
    fsdp_count = lax.axis_size("fsdp")
    seq_index = lax.axis_index("seq")
    fsdp_index = lax.axis_index("fsdp")
    row_count = tokens.shape[1]
    model_width = tokens.shape[2]
    length_total = segments.shape[1]
    heads_here = H // seq_count
    group_width = heads_here * HD
    block_size = min(512, length_total)
    score_scale = HD ** (-0.5)
    tokens_total = row_count * seq_count * fsdp_count
    full_qkv, full_out, full_bias, gain_one, shift_one, gain_two, shift_two = (
        lax.all_gather(w_qkv, "fsdp", axis=0, tiled=True),
        lax.all_gather(w_out, "fsdp", axis=0, tiled=True),
        lax.all_gather(b_qkv, "fsdp", axis=0, tiled=True),
        lax.all_gather(ln1_gain, "fsdp", axis=0, tiled=True),
        lax.all_gather(ln1_bias, "fsdp", axis=0, tiled=True),
        lax.all_gather(ln2_gain, "fsdp", axis=0, tiled=True),
        lax.all_gather(ln2_bias, "fsdp", axis=0, tiled=True),
    )
    gain_one = gain_one.astype(jnp.float32)
    gain_two = gain_two.astype(jnp.float32)
    segment = segments[0]
    positions_all = doc_positions(segment)
    positions = lax.dynamic_slice_in_dim(positions_all, seq_index * row_count, row_count, 0)
    tokens_in = tokens[0].astype(jnp.float32)
    teacher_in = teacher[0].astype(jnp.float32)
    counted = valid[0].astype(jnp.float32)
    normed_one, inv_std_one = norm_parts(tokens_in)
    hidden_one = (normed_one * gain_one + shift_one.astype(jnp.float32)).astype(jnp.bfloat16)
    qkv_float = jnp.dot(
        hidden_one, full_qkv, preferred_element_type=jnp.float32
    ) + full_bias.astype(jnp.float32)
    split_rows = qkv_float.reshape(row_count, 3, H, HD)
    packed = jnp.stack(
        [
            rotate(split_rows[:, 0], positions, 1.0),
            rotate(split_rows[:, 1], positions, 1.0),
            split_rows[:, 2],
        ],
        axis=1,
    )
    packed = packed.astype(jnp.bfloat16).reshape(row_count, 3, seq_count, group_width)
    spread = lax.all_to_all(packed, "seq", split_axis=2, concat_axis=0, tiled=True)
    head_rows = spread.reshape(length_total, 3, heads_here, HD)
    query_rows = head_rows[:, 0]
    key_rows = head_rows[:, 1]
    value_rows = head_rows[:, 2]
    heads_out, log_totals = attention_forward(
        query_rows, key_rows, value_rows, segment, block_size, score_scale
    )
    returned = lax.all_to_all(
        heads_out.reshape(length_total, 1, group_width),
        "seq",
        split_axis=0,
        concat_axis=1,
        tiled=True,
    )
    attn_rows = returned.reshape(row_count, model_width)
    resid = tokens_in + jnp.dot(attn_rows, full_out, preferred_element_type=jnp.float32)
    normed_two, inv_std_two = norm_parts(resid)
    hidden_two = (normed_two * gain_two + shift_two.astype(jnp.float32)).astype(jnp.bfloat16)
    piece_gate = lax.all_gather(w_gate_up, "fsdp", axis=0, tiled=True)
    piece_down = lax.all_gather(w_down, "fsdp", axis=0, tiled=True)
    gate_up = jnp.einsum("td,ukd->tku", hidden_two, piece_gate, preferred_element_type=jnp.float32)
    hidden_piece = (jax.nn.silu(gate_up[:, 0]) * gate_up[:, 1]).astype(jnp.bfloat16)
    running = jnp.dot(hidden_piece, piece_down, preferred_element_type=jnp.float32)
    outputs = resid + running
    differ = outputs - teacher_in
    cot = counted[:, None] * differ
    half_sum = 0.5 * jnp.sum(cot * differ)
    count_here = jnp.sum(counted)
    cot_low = cot.astype(jnp.bfloat16)
    piece_gate = lax.all_gather(w_gate_up, "fsdp", axis=0, tiled=True)
    piece_down = lax.all_gather(w_down, "fsdp", axis=0, tiled=True)
    hidden_grad = jnp.einsum("tc,uc->tu", cot_low, piece_down, preferred_element_type=jnp.float32)
    piece_grads = gate_backward(gate_up, hidden_grad)
    grad_running = jnp.einsum(
        "tku,ukd->td", piece_grads, piece_gate, preferred_element_type=jnp.float32
    )

    def unit_rows(first_row, row_total):
        gate_term = jnp.einsum(
            "tku,td->ukd", piece_grads, hidden_two, preferred_element_type=jnp.float32
        )
        down_term = jnp.einsum(
            "tu,td->ud", hidden_piece, cot_low, preferred_element_type=jnp.float32
        )
        return jnp.concatenate([gate_term, down_term[:, None]], axis=1)

    ff_shard = reduce_rows(unit_rows, w_down.shape[0])
    resid_grad = cot + norm_back(grad_running, normed_two, inv_std_two, gain_two)
    gain_two_grad = jnp.sum(grad_running * normed_two, axis=0)
    shift_two_grad = jnp.sum(grad_running, axis=0)
    resid_low = resid_grad.astype(jnp.bfloat16)
    out_grad = jnp.einsum(
        "tc,ec->te", resid_low, full_out, preferred_element_type=jnp.float32
    ).astype(jnp.bfloat16)
    head_grad = lax.all_to_all(
        out_grad.reshape(row_count, seq_count, group_width),
        "seq",
        split_axis=1,
        concat_axis=0,
        tiled=True,
    )
    head_grad = head_grad.reshape(length_total, heads_here, HD)
    query_grad, key_grad, value_grad = attention_backward(
        query_rows, key_rows, value_rows, head_grad, log_totals, segment, block_size, score_scale
    )
    back_packed = jnp.stack(
        [
            rotate(query_grad, positions_all, -1.0),
            rotate(key_grad, positions_all, -1.0),
            value_grad,
        ],
        axis=1,
    )
    back_packed = back_packed.astype(jnp.bfloat16).reshape(length_total, 3, 1, group_width)
    qkv_grad = lax.all_to_all(back_packed, "seq", split_axis=0, concat_axis=2, tiled=True).reshape(
        row_count, 3 * model_width
    )
    grad_one = jnp.einsum("tc,ec->te", qkv_grad, full_qkv, preferred_element_type=jnp.float32)
    tokens_grad = resid_grad + norm_back(grad_one, normed_one, inv_std_one, gain_one)
    gain_one_grad = jnp.sum(grad_one * normed_one, axis=0)
    shift_one_grad = jnp.sum(grad_one, axis=0)
    bias_grad = jnp.sum(qkv_grad.astype(jnp.float32), axis=0)

    def feature_rows(first_row, row_total):
        qkv_term = jnp.einsum("tr,tc->rc", hidden_one, qkv_grad, preferred_element_type=jnp.float32)
        out_term = jnp.einsum("tr,tc->rc", attn_rows, resid_low, preferred_element_type=jnp.float32)
        return jnp.concatenate([qkv_term, out_term], axis=1)

    attn_shard = reduce_rows(feature_rows, w_qkv.shape[0])
    attn_total, ff_total = (
        lax.psum(attn_shard.astype(jnp.bfloat16), "seq").astype(jnp.float32),
        lax.psum(ff_shard.astype(jnp.bfloat16), "seq").astype(jnp.float32),
    )
    (
        sum_half,
        sum_count,
        total_gain_one,
        total_shift_one,
        total_gain_two,
        total_shift_two,
        total_bias,
    ) = lax.psum(
        (
            half_sum,
            count_here,
            gain_one_grad,
            shift_one_grad,
            gain_two_grad,
            shift_two_grad,
            bias_grad,
        ),
        ("seq", "fsdp"),
    )
    factor = tokens_total / sum_count
    loss = 2.0 * sum_half / (sum_count * model_width)

    def own_part(total_vec):
        share = total_vec.shape[0] // fsdp_count
        return factor * lax.dynamic_slice_in_dim(total_vec, fsdp_index * share, share, 0)

    layer_out = outputs.astype(jnp.bfloat16)[None]
    grad_tokens = (factor * tokens_grad).astype(jnp.bfloat16)[None]
    return (
        layer_out,
        loss,
        grad_tokens,
        own_part(total_gain_one),
        own_part(total_shift_one),
        factor * attn_total[:, : 3 * model_width],
        own_part(total_bias),
        factor * attn_total[:, 3 * model_width :],
        own_part(total_gain_two),
        own_part(total_shift_two),
        factor * ff_total[:, :2],
        factor * ff_total[:, 2],
    )


def solution(mesh):
    placed = (
        P("fsdp", "seq", None),
        P("fsdp", "seq", None),
        P("fsdp", None),
        P("fsdp", "seq"),
        P("fsdp"),
        P("fsdp"),
        P("fsdp", None),
        P("fsdp"),
        P("fsdp", None),
        P("fsdp"),
        P("fsdp"),
        P("fsdp", None, None),
        P("fsdp", None),
    )
    return jax.shard_map(
        per_device,
        mesh=mesh,
        in_specs=placed,
        out_specs=(
            P("fsdp", "seq", None),
            P(),
            P("fsdp", "seq", None),
            P("fsdp"),
            P("fsdp"),
            P("fsdp", None),
            P("fsdp"),
            P("fsdp", None),
            P("fsdp"),
            P("fsdp"),
            P("fsdp", None, None),
            P("fsdp", None),
        ),
        check_vma=False,
    )
```

profile of v0, /device:TPU:0, one launch (start us, length us, event | category | flops | bytes accessed | tf_op | source)
XLA Modules:
  0.0 4082.9 jit_solution(5188963605835579992)
XLA Ops:
  8.7 7.8 copy.122
  17.8 48.8 %all-gather.1 = bf16[8,1,256]{2,1,0:T(2,128)(2,1)S(1)} all-gather(bf16[1,1,256]{2,1,0:T(2,128)(2,1)S(1)} %reshape.465), channel_id=1, replica_groups=mesh['seq'=4,'fsdp'=8] {'fsdp'}, dimensions={0}, use_global_device_ids=true | all-gather | bytes 4608 | tf_op jit(solution)/shard_map/all_gather | solution.py:180
  66.6 30.9 all-gather
  97.5 39.9 all-gather.2
  139.2 354.2 %all-gather.10.cloned.1.call-done = bf16[2048,6144]{1,0:T(8,128)(2,1)} async-done(((bf16[256,6144]{1,0:T(8,128)(2,1)}), bf16[2048,6144]{1,0:T(8,128)(2,1)}) %all-gather.10.cloned.1.call-update) | async-done | bytes 25165840 | tf_op jit(solution)/shard_map/all_gather | solution.py:176
  493.4 13.4 convolution_add_fusion
  506.8 6.6 copy.116
  524.5 36.8 all-to-all-done
  565.4 6.1 reshape.456
  575.3 37.4 while.27
  579.2 4.7 fusion.125
  583.9 4.2 fusion.126
  588.1 5.9 fusion.127
  597.9 4.7 fusion.125
  602.6 4.2 fusion.126
  606.8 5.9 fusion.127
  615.3 7.2 reshape.481
  623.0 8.1 reduce.8
  638.5 64.3 %all-gather.4 = bf16[8,1,256]{2,1,0:T(2,128)(2,1)S(1)} all-gather(bf16[1,1,256]{2,1,0:T(2,128)(2,1)S(1)} %reshape.471), channel_id=1, replica_groups=mesh['seq'=4,'fsdp'=8] {'fsdp'}, dimensions={0}, use_global_device_ids=true | all-gather | bytes 4608 | tf_op jit(solution)/shard_map/all_gather | solution.py:182
  702.8 30.6 all-gather.3
  739.2 6.3 fusion.77
  745.9 748.3 %all-gather.14.cloned.1.call-done = bf16[5632,2,2048]{2,0,1:T(8,128)(2,1)} async-done(((bf16[704,2,2048]{2,0,1:T(8,128)(2,1)}), bf16[5632,2,2048]{2,0,1:T(8,128)(2,1)}) %all-gather.14.cloned.1.call-update) | async-done | bytes 46137360 | tf_op jit(solution)/shard_map/all_gather | solution.py:226
  1494.3 23.7 convolution_bitcast_fusion
  1518.0 6.3 multiply_convert_fusion.2
  1524.3 412.4 %all-gather.16.cloned.1.call-done = bf16[5632,2048]{1,0:T(8,128)(2,1)} async-done(((bf16[704,2048]{1,0:T(8,128)(2,1)}), bf16[5632,2048]{1,0:T(8,128)(2,1)}) %all-gather.16.cloned.1.call-update) | async-done | bytes 23068688 | tf_op jit(solution)/shard_map/all_gather | solution.py:227
  1936.7 12.5 multiply_convert_fusion.3
  1949.2 12.6 convert_bitcast_fusion.1
  1961.9 25.6 fusion.31
  1987.4 21.2 convert_bitcast_fusion
  2008.6 46.8 %pad_maximum_fusion = bf16[5632,3,2048]{0,2,1:T(8,128)(2,1)} fusion(bf16[5632,1,2048]{0,2,1:T(8,128)(2,1)} %convert_bitcast_fusion.1, bf16[5632,2,2048]{0,2,1:T(8,128)(2,1)} %convert_bitcast_fusion), kind=kLoop, calls=%fused_computation.40 | loop fusion | flops 34603008 | bytes 138412032 | tf_op jit(solution)/shard_map/concatenate | solution.py:252
  2055.4 88.8 %copy.142 = bf16[5632,6144]{1,0:T(8,128)(2,1)} copy(bf16[5632,6144]{0,1:T(8,128)(2,1)} %bitcast.64) | data formatting | bytes 138412032
  2144.3 22.0 multiply_reduce_fusion.1
  2169.4 6.5 convolution_convert_fusion.2
  2181.6 13.5 all-to-all-done.2
  2197.4 154.1 %while.28 = (s32[]{:T(128)}, f32[1024,8,64]{0,2,1:T(8,128)}, f32[1024,8,64]{0,2,1:T(8,128)}, f32[2,512,8,64]{1,0,3,2:T(2,128)}, s32[2]{0:T(128)S(1)}, /*index=5*...) while((s32[]{:T(128)}, f32[1024,8,64]{0,2,1:T(8,128)}, ...), condition=%wide.region_18.19_spmd.clone, body=%wide.region_16.18_spmd.clone.sunk | while | flops 2726556160 | bytes 233929072 | solution.py:133
  2201.5 9.8 fusion.137
  2211.3 13.8 multiply_reduce_fusion.7
  2225.1 11.9 multiply_convert_fusion.5
  2254.5 19.7 dynamic_update_slice.20
  2278.0 9.8 fusion.137
  2287.8 13.9 multiply_reduce_fusion.7
  2301.7 11.7 multiply_convert_fusion.5
  2317.5 4.7 bitcast_add_fusion.5
  2331.7 19.6 dynamic_update_slice.20
  2351.5 4.2 reshape.460
  2359.9 5.7 copy.126
  2365.6 5.1 all-to-all-start.3
  2370.8 5.7 convolution_convert_fusion.1
  2376.5 42.4 %all-to-all-done.3 = bf16[1024,3,1,512]{3,1,2,0:T(4,128)(2,1)} async-done(((bf16[1024,3,1,512]{3,1,2,0:T(4,128)(2,1)}), bf16[1024,3,1,512]{3,1,2,0:T(4,128)(2,1)}, u32[]{:S(2)}, u32[]{:S(2)}) %all-to-all-start.3) | async-done | bytes 3145760 | tf_op jit(solution)/shard_map/all_to_all | solution.py:282
  2418.9 4.7 copy.127
  2423.7 4.8 copy.128
  2428.5 14.3 convolution_convert_fusion
  2442.9 22.9 pad_maximum_fusion.1
  2465.8 764.0 %reduce-scatter.7.cloned.1.call-done = bf16[704,6144]{1,0:T(8,128)(2,1)} async-done(((bf16[5632,6144]{1,0:T(8,128)(2,1)}), bf16[704,6144]{1,0:T(8,128)(2,1)}) %reduce-scatter.7.cloned.1.call-update) | async-done | bytes 8650768
  3229.8 12.8 copy.143
  3242.6 529.5 %reduce-scatter.5.cloned.1.call-done = bf16[256,8192]{1,0:T(8,128)(2,1)} async-done(((bf16[2048,8192]{1,0:T(8,128)(2,1)}), bf16[256,8192]{1,0:T(8,128)(2,1)}) %reduce-scatter.5.cloned.1.call-update) | async-done | bytes 4194320 | tf_op jit(solution)/shard_map/reduce_scatter | solution.py:140
  3776.4 15.2 fusion.49
  3791.6 41.5 %all-reduce = (f32[]{:T(128)}, f32[]{:T(128)}, f32[2048]{0:T(1024)S(1)}, f32[2048]{0:T(1024)S(1)}, f32[6144]{0:T(1024)S(1)}, /*index=5*/f32[2048]{0:T(1024)S(1)}, f32[2048]{0:T(1024)S(1)}) all-reduce(f32[]{:T(128)S(6)} %mul_shard_map.3, f32[]{:T(128)} %convert_reduce_fusion.2, ...), channel_id=1, replica_groups=mesh['seq'=4,'fsdp'=8] {'seq','fsdp'}, use_global_device_ids=true, to_apply=%region_11.12 | all-reduce | flops 14338 | bytes 114704 | tf_op jit(solution)/shard_map/psum | solution.py:309
  3841.8 171.7 %all-reduce.4.cloned.1.call-done = (bf16[256,8192]{1,0:T(8,128)(2,1)}, bf16[704,3,2048]{0,2,1:T(8,128)(2,1)}) async-done(((bf16[256,8192]{1,0:T(8,128)(2,1)}, bf16[704,3,2048]{0,2,1:T(8,128)(2,1)}), (bf16[256,8192]{1,0:T(8,128)(2,1)}, bf16[704,3,2048]{0,2,1:T(8,128)(2,1)})) %all-reduce.4.cloned.1.call-update) | async-done | bytes 12845072 | tf_op jit(solution)/shard_map/psum | solution.py:298
  4021.3 11.8 convert_element_type.146
  4033.1 5.9 fusion.27
  4039.0 10.0 slice_multiply_fusion
  4049.0 19.1 copy.132
  4068.1 6.4 copy.133
  (228 shorter events, 111.9 us)
Async XLA Ops:
  7.2 486.2 %all-gather.10.cloned.1.call-start = ((), (), s32[]{:S(2)}) async-start(), calls=%async_computation.6 | async-start | bytes 28311552 | tf_op jit(solution)/shard_map/all_gather | solution.py:176
  7.9 731.3 %all-gather.12.cloned.1.call-start = ((), (), s32[]{:S(2)}) async-start(), calls=%async_computation.7 | async-start | bytes 9437184 | tf_op jit(solution)/shard_map/all_gather | solution.py:177
  8.7 1485.6 %all-gather.14.cloned.1.call-start = ((), (), s32[]{:S(2)}) async-start(), calls=%async_computation.8 | async-start | bytes 51904512 | tf_op jit(solution)/shard_map/all_gather | solution.py:226
  16.5 0.7 copy-start.42
  16.5 0.7 copy-start.43
  16.5 0.7 copy-start.39
  16.5 0.7 copy-start.15
  16.5 121.9 %copy-start.8 = (bf16[1,256,2048]{2,1,0:T(8,128)(2,1)S(1)}, bf16[1,256,2048]{2,1,0:T(8,128)(2,1)}, u32[]{:S(2)}) copy-start(bf16[1,256,2048]{2,1,0:T(8,128)(2,1)} %param.17) | copy-start | bytes 3145732
  16.6 1920.1 %all-gather.16.cloned.1.call-start = ((), (), s32[]{:S(2)}) async-start(), calls=%async_computation.9 | async-start | bytes 25952256 | tf_op jit(solution)/shard_map/all_gather | solution.py:227
  66.6 440.2 %copy-start.22 = (f32[8,1,256]{2,1,0:T(1,128)}, f32[8,1,256]{2,1,0:T(1,128)S(1)}, u32[]{:S(2)}) copy-start(f32[8,1,256]{2,1,0:T(1,128)S(1)} %convert_element_type.149) | copy-start | bytes 24580
  97.5 409.3 %copy-start.20 = (f32[8,1,256]{2,1,0:T(1,128)}, f32[8,1,256]{2,1,0:T(1,128)S(1)}, u32[]{:S(2)}) copy-start(f32[8,1,256]{2,1,0:T(1,128)S(1)} %convert_element_type.148) | copy-start | bytes 24580
  137.5 369.3 %copy-start.37 = (f32[8]{0:T(128)}, f32[8]{0:T(128)S(1)}, u32[]{:S(2)}) copy-start(f32[8]{0:T(128)S(1)} %multiply_power_fusion) | copy-start | bytes 100
  138.6 368.2 %copy-start.28 = (f32[256]{0:T(256)}, f32[256]{0:T(256)S(1)}, u32[]{:S(2)}) copy-start(f32[256]{0:T(256)S(1)} %broadcast_multiply_fusion.5) | copy-start | bytes 3076
  139.0 367.8 %copy-start.30 = (f32[256]{0:T(256)}, f32[256]{0:T(256)S(1)}, u32[]{:S(2)}) copy-start(f32[256]{0:T(256)S(1)} %add_rsqrt_fusion.1) | copy-start | bytes 3076
  520.6 40.8 all-to-all-start
  571.5 3.8 copy-start.19
  612.8 9.7 copy-start.24
  612.8 9.7 copy-start.46
  612.8 125.1 %copy-start.1 = (bf16[1024,8,64]{0,2,1:T(8,128)(2,1)}, bf16[1024,8,64]{0,2,1:T(8,128)(2,1)S(1)}, u32[]{:S(2)}) copy-start(bf16[1024,8,64]{0,2,1:T(8,128)(2,1)S(1)} %get-tuple-element.590) | copy-start | bytes 3145732
  623.0 15.4 copy-start.44
  623.0 15.4 copy-start.45
  623.0 15.5 copy-start.40
  634.8 98.6 %all-to-all-start.1 = ((bf16[4,2,65536]{2,1,0:T(2,128)(2,1)}), bf16[4,2,65536]{2,1,0:T(2,128)(2,1)S(1)}, u32[]{:S(2)}, u32[]{:S(2)}) async-start(bf16[4,2,65536]{2,1,0:T(2,128)(2,1)} %reshape.486), calls=%async_computation.1 | async-start | bytes 2097152 | tf_op jit(solution)/shard_map/all_to_all | solution.py:215
  638.4 2591.4 %reduce-scatter.7.cloned.1.call-start = ((), (), s32[]{:S(2)}) async-start(), calls=%async_computation.11 | async-start | bytes 77856768
  638.5 1298.2 %copy-start.35 = (f32[1,256]{1,0:T(1,128)}, f32[1,256]{1,0:T(1,128)S(1)}, u32[]{:S(2)}) copy-start(f32[1,256]{1,0:T(1,128)S(1)} %convert_element_type.133) | copy-start | bytes 3076
  735.9 3.3 copy-start.9
  1518.0 418.7 %copy-start.17 = (bf16[1,256,2048]{2,1,0:T(8,128)(2,1)S(1)}, bf16[1,256,2048]{2,1,0:T(8,128)(2,1)}, u32[]{:S(2)}) copy-start(bf16[1,256,2048]{2,1,0:T(8,128)(2,1)} %param.18) | copy-start | bytes 3145732
  2144.2 22.0 copy-start.14
  2144.2 22.0 copy-start.18
  2144.3 22.0 copy-start.36
  2169.4 6.6 copy-start.11
  2176.0 4.8 copy-start.32
  2176.0 4.8 copy-start.38
  2177.1 20.3 copy-start.2
  2177.1 20.3 copy-start.16
  2177.1 20.3 copy-start.25
  2177.1 20.3 copy-start.47
  2177.1 18.1 all-to-all-start.2
  2225.1 15.9 copy-start
  2245.0 4.1 copy-start.4
  2252.1 1.3 copy-start.5
  2253.4 20.7 copy-start.3
  2301.7 15.8 copy-start
  2322.3 4.0 copy-start.4
  2329.3 1.3 copy-start.5
  2330.6 20.7 copy-start.3
  2351.5 4.2 copy-start.6
  2355.7 2.2 copy-start.7
  2355.7 2.4 copy-start.26
  2355.7 2.4 copy-start.27
  2365.6 5.2 copy-start.12
  2365.6 5.2 copy-start.13
  2365.6 53.3 %all-to-all-start.3 = ((bf16[1024,3,1,512]{3,1,2,0:T(4,128)(2,1)}), bf16[1024,3,1,512]{3,1,2,0:T(4,128)(2,1)}, u32[]{:S(2)}, u32[]{:S(2)}) async-start(bf16[1024,3,1,512]{3,1,2,0:T(4,128)(2,1)} %copy.126), calls=%async_computation.3 | async-start | bytes 8388608 | tf_op jit(solution)/shard_map/all_to_all | solution.py:282
  2370.7 1401.4 %reduce-scatter.5.cloned.1.call-start = ((), (), s32[]{:S(2)}) async-start(), calls=%async_computation.10 | async-start | bytes 37748736 | tf_op jit(solution)/shard_map/reduce_scatter | solution.py:140
  2423.7 4.8 copy-start.10
  2423.7 4.8 copy-start.21
  2423.7 4.8 copy-start.23
  2423.7 4.8 copy-start.29
  2423.7 4.8 copy-start.31
  2465.8 1547.7 %all-reduce.4.cloned.1.call-start = ((), (), s32[]{:S(2)}) async-start(), calls=%async_computation.12 | async-start | bytes 27262976 | tf_op jit(solution)/shard_map/psum | solution.py:298
  3772.1 0.7 copy-start.41
  3776.4 15.2 copy-start.33
  3776.4 15.2 copy-start.34
Sparse Core Ops, SparseCore 0:
  9.5 483.8 all-gather.9
  495.5 124.4 all-gather.11
  622.1 872.0 all-gather.13
  1495.6 441.0 all-gather.15
  2144.4 1085.4 reduce-scatter.6
  3233.5 538.6 reduce-scatter.4
  3775.3 238.1 all-reduce.3
where the time goes:
time: 4100 us; the launch traced here: 4080 us
  waiting for transfers between devices  3070 us (75%)
  matrix products  270 us (7%)
  local copies, waits for them, and re-layouts  262 us (6%)
  blocking collectives  256 us (6%)
  other arithmetic  175 us (4%)
    unnamed x8, waiting for transfers between devices  766 us
    all_gather x1, waiting for transfers between devices, per_device(): piece_gate = lax.all_gather(w_gate_up, 'fsdp', axis=0, tiled=True)  748 us
    reduce_scatter x1, waiting for transfers between devices, reduce_rows(): lax.psum_scatter(term_rows(jnp.int32(0), row_share * lax.axis_size('fsdp'...  530 us
    all_gather x1, waiting for transfers between devices, per_device(): piece_down = lax.all_gather(w_down, 'fsdp', axis=0, tiled=True)  412 us
    all_gather x1, waiting for transfers between devices, per_device(): lax.all_gather(w_qkv, 'fsdp', axis=0, tiled=True)  354 us
    psum x1, waiting for transfers between devices, per_device(): lax.psum(attn_shard.astype(jnp.bfloat16), 'seq').astype(jnp.float32)  172 us
    unnamed x102, local copies, waits for them, and re-layouts  144 us
  transfers between devices with their start and end apart: 11, of which 9 were waited for; matrix products, arithmetic and copies ran while one was open for 10% of the time, Pallas kernels for 0%

commit v1 on v0

--- a/solution.py
+++ b/solution.py
@@ -295,7 +295,7 @@
 
     attn_shard = reduce_rows(feature_rows, w_qkv.shape[0])
     attn_total, ff_total = (
-        lax.psum(attn_shard.astype(jnp.bfloat16), "seq").astype(jnp.float32),
+        jnp.sum(lax.all_gather(attn_shard.astype(jnp.bfloat16), "seq"), axis=0).astype(jnp.float32),
         lax.psum(ff_shard.astype(jnp.bfloat16), "seq").astype(jnp.float32),
     )
     (

time: 4100 us -> 4270 us (1.041)
  waiting for transfers between devices: 3070 us -> 3240 us
    unnamed x8 -> x9, waiting for transfers between devices: 766 us -> 1090 us
    reduce_scatter x1, waiting for transfers between devices: 530 us -> 367 us  [reduce_rows(): lax.psum_scatter(term_rows(jnp.int32(0), row_share * lax.axis_size('fsdp'...]
    unnamed x102 -> x112, local copies, waits for them, and re-layouts: 144 us -> 146 us
  transfers between devices with their start and end apart: 11 -> 12, of which waited for: 9 -> 10; matrix products, arithmetic and copies ran while one was open for 10% -> 9% of each run, Pallas kernels for 0% -> 0%
where the time goes in v1:
time: 4270 us; the launch traced here: 4250 us
  waiting for transfers between devices  3240 us (76%)
  local copies, waits for them, and re-layouts  264 us (6%)
  matrix products  259 us (6%)
  blocking collectives  256 us (6%)
  other arithmetic  189 us (4%)
    unnamed x9, waiting for transfers between devices  1090 us
    all_gather x1, waiting for transfers between devices, per_device(): piece_gate = lax.all_gather(w_gate_up, 'fsdp', axis=0, tiled=True)  747 us
    all_gather x1, waiting for transfers between devices, per_device(): piece_down = lax.all_gather(w_down, 'fsdp', axis=0, tiled=True)  412 us
    reduce_scatter x1, waiting for transfers between devices, reduce_rows(): lax.psum_scatter(term_rows(jnp.int32(0), row_share * lax.axis_size('fsdp'...  367 us
    all_gather x1, waiting for transfers between devices, per_device(): lax.all_gather(w_qkv, 'fsdp', axis=0, tiled=True)  354 us
    psum x1, waiting for transfers between devices, per_device(): lax.psum(ff_shard.astype(jnp.bfloat16), 'seq').astype(jnp.float32)  153 us
    unnamed x112, local copies, waits for them, and re-layouts  146 us
  transfers between devices with their start and end apart: 12, of which 10 were waited for; matrix products, arithmetic and copies ran while one was open for 9% of the time, Pallas kernels for 0%

profile of v1, /device:TPU:0, one launch (start us, length us, event | category | flops | bytes accessed | tf_op | source)
XLA Modules:
  0.0 4251.9 jit_solution(8990087259115370802)
XLA Ops:
  8.7 7.8 copy.122
  17.8 48.8 %all-gather.2 = bf16[8,1,256]{2,1,0:T(2,128)(2,1)S(1)} all-gather(bf16[1,1,256]{2,1,0:T(2,128)(2,1)S(1)} %reshape.466), channel_id=1, replica_groups=mesh['seq'=4,'fsdp'=8] {'fsdp'}, dimensions={0}, use_global_device_ids=true | all-gather | bytes 4608 | tf_op jit(solution)/shard_map/all_gather | solution.py:180
  66.6 30.9 all-gather.1
  97.5 39.9 all-gather.3
  139.2 354.2 %all-gather.12.cloned.1.call-done = bf16[2048,6144]{1,0:T(8,128)(2,1)} async-done(((bf16[256,6144]{1,0:T(8,128)(2,1)}), bf16[2048,6144]{1,0:T(8,128)(2,1)}) %all-gather.12.cloned.1.call-update) | async-done | bytes 25165840 | tf_op jit(solution)/shard_map/all_gather | solution.py:176
  493.4 13.4 convolution_add_fusion
  506.9 6.6 copy.116
  524.6 36.8 all-to-all-done
  565.5 6.1 reshape.456
  575.3 37.4 while.27
  579.2 4.7 fusion.125
  588.1 5.9 fusion.127
  597.9 4.7 fusion.125
  602.6 4.2 fusion.126
  606.8 5.9 fusion.127
  615.3 7.2 reshape.482
  622.9 8.1 reduce.9
  639.1 63.7 %all-gather.5 = bf16[8,1,256]{2,1,0:T(2,128)(2,1)S(1)} all-gather(bf16[1,1,256]{2,1,0:T(2,128)(2,1)S(1)} %reshape.472), channel_id=1, replica_groups=mesh['seq'=4,'fsdp'=8] {'fsdp'}, dimensions={0}, use_global_device_ids=true | all-gather | bytes 4608 | tf_op jit(solution)/shard_map/all_gather | solution.py:182
  702.8 30.6 all-gather.4
  739.8 6.5 fusion.77
  746.8 747.5 %all-gather.16.cloned.1.call-done = bf16[5632,2,2048]{2,0,1:T(8,128)(2,1)} async-done(((bf16[704,2,2048]{2,0,1:T(8,128)(2,1)}), bf16[5632,2,2048]{2,0,1:T(8,128)(2,1)}) %all-gather.16.cloned.1.call-update) | async-done | bytes 46137360 | tf_op jit(solution)/shard_map/all_gather | solution.py:226
  1494.3 23.7 convolution_bitcast_fusion
  1518.0 6.3 multiply_convert_fusion.2
  1524.3 412.4 %all-gather.18.cloned.1.call-done = bf16[5632,2048]{1,0:T(8,128)(2,1)} async-done(((bf16[704,2048]{1,0:T(8,128)(2,1)}), bf16[5632,2048]{1,0:T(8,128)(2,1)}) %all-gather.18.cloned.1.call-update) | async-done | bytes 23068688 | tf_op jit(solution)/shard_map/all_gather | solution.py:227
  1936.7 12.5 multiply_convert_fusion.3
  1949.2 17.7 fusion.31
  1966.9 21.7 multiply_reduce_fusion.1
  1988.6 4.4 multiply_add_fusion
  2000.9 13.5 all-to-all-done.2
  2016.7 152.0 %while.28 = (s32[]{:T(128)}, f32[1024,8,64]{0,2,1:T(8,128)}, f32[1024,8,64]{0,2,1:T(8,128)}, f32[2,512,8,64]{1,0,3,2:T(2,128)}, s32[2]{0:T(128)S(1)}, /*index=5*...) while((s32[]{:T(128)}, f32[1024,8,64]{0,2,1:T(8,128)}, ...), condition=%wide.region_18.19_spmd.clone, body=%wide.region_16.18_spmd.clone.sunk | while | flops 2726556160 | bytes 238123408 | solution.py:133
  2020.7 9.6 fusion.137
  2030.3 13.6 multiply_reduce_fusion.7
  2043.9 11.5 multiply_convert_fusion.5
  2072.8 19.6 dynamic_update_slice.20
  2096.3 9.6 fusion.137
  2105.9 13.6 multiply_reduce_fusion.7
  2119.5 11.5 multiply_convert_fusion.5
  2134.8 4.7 bitcast_add_fusion.5
  2149.0 19.6 dynamic_update_slice.20
  2176.9 5.7 copy.126
  2182.6 5.1 all-to-all-start.3
  2187.8 5.7 convolution_convert_fusion.1
  2193.5 42.4 all-to-all-done.3
  2235.9 4.6 copy.127
  2240.6 4.7 copy.128
  2245.3 13.9 convolution_convert_fusion
  2259.2 22.9 pad_maximum_fusion.1
  2283.4 12.8 convert_bitcast_fusion.1
  2296.2 21.3 convert_bitcast_fusion
  2317.5 47.1 %pad_maximum_fusion = bf16[5632,3,2048]{0,2,1:T(8,128)(2,1)} fusion(bf16[5632,1,2048]{0,2,1:T(8,128)(2,1)} %convert_bitcast_fusion.1, bf16[5632,2,2048]{0,2,1:T(8,128)(2,1)} %convert_bitcast_fusion), kind=kLoop, calls=%fused_computation.40 | loop fusion | flops 34603008 | bytes 138412032 | tf_op jit(solution)/shard_map/concatenate | solution.py:252
  2364.7 89.0 %copy.142 = bf16[5632,6144]{1,0:T(8,128)(2,1)} copy(bf16[5632,6144]{0,1:T(8,128)(2,1)} %bitcast.65) | data formatting | bytes 138412032
  2453.8 366.6 %reduce-scatter.5.cloned.1.call-done = bf16[256,8192]{1,0:T(8,128)(2,1)} async-done(((bf16[2048,8192]{1,0:T(8,128)(2,1)}), bf16[256,8192]{1,0:T(8,128)(2,1)}) %reduce-scatter.5.cloned.1.call-update) | async-done | bytes 4194320 | tf_op jit(solution)/shard_map/reduce_scatter | solution.py:140
  2821.7 1086.9 %reduce-scatter.7.cloned.1.call-done = bf16[704,6144]{1,0:T(8,128)(2,1)} async-done(((bf16[5632,6144]{1,0:T(8,128)(2,1)}), bf16[704,6144]{1,0:T(8,128)(2,1)}) %reduce-scatter.7.cloned.1.call-update) | async-done | bytes 8650768
  3908.6 12.5 copy.143
  3922.7 16.6 fusion.49
  3941.8 42.3 all-reduce
  3992.9 24.5 all-gather.20.cloned.1.call-done
  4017.4 12.3 reduce_sum.179
  4037.5 152.8 %all-reduce.3.cloned.1.call-done = bf16[704,3,2048]{0,2,1:T(8,128)(2,1)} async-done(((bf16[704,3,2048]{0,2,1:T(8,128)(2,1)}), bf16[704,3,2048]{0,2,1:T(8,128)(2,1)}) %all-reduce.3.cloned.1.call-update) | async-done | bytes 8650768 | tf_op jit(solution)/shard_map/psum | solution.py:299
  4190.3 11.8 convert_element_type.148
  4202.1 5.9 fusion.27
  4208.0 10.0 slice_multiply_fusion
  4218.0 19.1 copy.132
  4237.1 6.4 copy.133
  (247 shorter events, 122.5 us)
Async XLA Ops:
  7.2 486.2 %all-gather.12.cloned.1.call-start = ((), (), s32[]{:S(2)}) async-start(), calls=%async_computation.6 | async-start | bytes 28311552 | tf_op jit(solution)/shard_map/all_gather | solution.py:176
  7.9 731.9 %all-gather.14.cloned.1.call-start = ((), (), s32[]{:S(2)}) async-start(), calls=%async_computation.7 | async-start | bytes 9437184 | tf_op jit(solution)/shard_map/all_gather | solution.py:177
  8.7 1485.6 %all-gather.16.cloned.1.call-start = ((), (), s32[]{:S(2)}) async-start(), calls=%async_computation.8 | async-start | bytes 51904512 | tf_op jit(solution)/shard_map/all_gather | solution.py:226
  16.5 121.9 %copy-start.9 = (bf16[1,256,2048]{2,1,0:T(8,128)(2,1)S(1)}, bf16[1,256,2048]{2,1,0:T(8,128)(2,1)}, u32[]{:S(2)}) copy-start(bf16[1,256,2048]{2,1,0:T(8,128)(2,1)} %param.17) | copy-start | bytes 3145732
  16.6 1920.1 %all-gather.18.cloned.1.call-start = ((), (), s32[]{:S(2)}) async-start(), calls=%async_computation.9 | async-start | bytes 25952256 | tf_op jit(solution)/shard_map/all_gather | solution.py:227
  66.6 440.2 %copy-start.28 = (f32[8,1,256]{2,1,0:T(1,128)}, f32[8,1,256]{2,1,0:T(1,128)S(1)}, u32[]{:S(2)}) copy-start(f32[8,1,256]{2,1,0:T(1,128)S(1)} %convert_element_type.151) | copy-start | bytes 24580
  97.5 409.3 %copy-start.23 = (f32[8,1,256]{2,1,0:T(1,128)}, f32[8,1,256]{2,1,0:T(1,128)S(1)}, u32[]{:S(2)}) copy-start(f32[8,1,256]{2,1,0:T(1,128)S(1)} %convert_element_type.150) | copy-start | bytes 24580
  137.5 369.4 %copy-start.43 = (f32[8]{0:T(128)}, f32[8]{0:T(128)S(1)}, u32[]{:S(2)}) copy-start(f32[8]{0:T(128)S(1)} %multiply_power_fusion) | copy-start | bytes 100
  138.6 368.3 %copy-start.34 = (f32[256]{0:T(256)}, f32[256]{0:T(256)S(1)}, u32[]{:S(2)}) copy-start(f32[256]{0:T(256)S(1)} %broadcast_multiply_fusion.5) | copy-start | bytes 3076
  139.0 367.8 %copy-start.37 = (f32[256]{0:T(256)}, f32[256]{0:T(256)S(1)}, u32[]{:S(2)}) copy-start(f32[256]{0:T(256)S(1)} %add_rsqrt_fusion.1) | copy-start | bytes 3076
  520.6 40.8 all-to-all-start
  571.5 3.8 copy-start.21
  622.9 16.1 copy-start.50
  622.9 16.1 copy-start.51
  622.9 16.1 copy-start.46
  634.8 98.7 %all-to-all-start.1 = ((bf16[4,2,65536]{2,1,0:T(2,128)(2,1)}), bf16[4,2,65536]{2,1,0:T(2,128)(2,1)}, u32[]{:S(2)}, u32[]{:S(2)}) async-start(bf16[4,2,65536]{2,1,0:T(2,128)(2,1)} %reshape.487), calls=%async_computation.1 | async-start | bytes 2097152 | tf_op jit(solution)/shard_map/all_to_all | solution.py:215
  702.8 791.5 %copy-start.18 = (f32[8,1,256]{2,1,0:T(1,128)}, f32[8,1,256]{2,1,0:T(1,128)S(1)}, u32[]{:S(2)}) copy-start(f32[8,1,256]{2,1,0:T(1,128)S(1)} %convert_element_type.154) | copy-start | bytes 24580
  733.5 1255.1 %copy-start.16 = (f32[8,1,256]{2,1,0:T(1,128)}, f32[8,1,256]{2,1,0:T(1,128)S(1)}, u32[]{:S(2)}) copy-start(f32[8,1,256]{2,1,0:T(1,128)S(1)} %convert_element_type.153) | copy-start | bytes 24580
  746.4 1242.2 %copy-start.7 = (f32[256,2048]{1,0:T(8,128)}, f32[256,2048]{1,0:T(8,128)S(1)}, u32[]{:S(2)}) copy-start(f32[256,2048]{1,0:T(8,128)S(1)} %get-tuple-element.354) | copy-start | bytes 6291460
  746.4 1242.2 %copy-start.26 = (f32[256]{0:T(256)}, f32[256]{0:T(256)S(1)}, u32[]{:S(2)}) copy-start(f32[256]{0:T(256)S(1)} %broadcast_multiply_fusion.4) | copy-start | bytes 3076
  746.8 1241.8 %copy-start.30 = (f32[256]{0:T(256)}, f32[256]{0:T(256)S(1)}, u32[]{:S(2)}) copy-start(f32[256]{0:T(256)S(1)} %add_rsqrt_fusion) | copy-start | bytes 3076
  1949.2 43.8 %slice-start = ((s8[8388608]{0:T(1024)(128)(4,1)}), s8[4194304]{0:T(1024)(128)(4,1)S(1)}, s32[]{:S(2)}) async-start(s8[8388608]{0:T(1024)(128)(4,1)} %bitcast.249), calls=%async_computation.14 | async-start | bytes 8388608
  1966.9 26.1 slice-start.1
  1993.0 2.5 copy-start.12
  1995.5 4.6 copy-start.40
  1995.5 4.6 copy-start.44
  1996.6 17.9 all-to-all-start.2
  2016.7 13.6 copy-start.1
  2043.9 15.4 copy-start
  2063.3 4.0 copy-start.3
  2071.7 20.7 copy-start.2
  2092.4 13.5 copy-start.1
  2119.5 15.4 copy-start
  2139.6 4.0 copy-start.3
  2147.9 20.7 copy-start.2
  2168.7 4.2 copy-start.5
  2172.9 2.1 copy-start.6
  2172.9 2.2 copy-start.32
  2172.9 2.2 copy-start.33
  2182.6 5.2 copy-start.13
  2182.6 5.2 copy-start.15
  2182.6 53.3 %all-to-all-start.3 = ((bf16[1024,3,1,512]{3,1,2,0:T(4,128)(2,1)}), bf16[1024,3,1,512]{3,1,2,0:T(4,128)(2,1)}, u32[]{:S(2)}, u32[]{:S(2)}) async-start(bf16[1024,3,1,512]{3,1,2,0:T(4,128)(2,1)} %copy.126), calls=%async_computation.3 | async-start | bytes 8388608 | tf_op jit(solution)/shard_map/all_to_all | solution.py:282
  2187.7 632.7 %reduce-scatter.5.cloned.1.call-start = ((), (), s32[]{:S(2)}) async-start(), calls=%async_computation.10 | async-start | bytes 37748736 | tf_op jit(solution)/shard_map/reduce_scatter | solution.py:140
  2240.6 4.7 copy-start.10
  2240.6 4.7 copy-start.24
  2240.6 4.7 copy-start.29
  2240.6 4.8 copy-start.35
  2240.6 4.8 copy-start.38
  2282.2 14.0 copy-start.8
  2282.2 14.0 copy-start.17
  2282.2 14.0 copy-start.19
  2282.2 14.0 copy-start.27
  2282.2 14.0 copy-start.31
  2282.2 1626.4 %reduce-scatter.7.cloned.1.call-start = ((), (), s32[]{:S(2)}) async-start(), calls=%async_computation.13 | async-start | bytes 77856768
  2453.7 366.8 %copy-start.47 = (s32[1,256]{1,0:T(1,128)S(1)}, s32[1,256]{1,0:T(1,128)}, u32[]{:S(2)}) copy-start(s32[1,256]{1,0:T(1,128)} %param.20) | copy-start | bytes 3076
  2453.7 1563.7 %all-gather.20.cloned.1.call-start = ((), (), s32[]{:S(2)}) async-start(), calls=%async_computation.12 | async-start | bytes 20971520 | tf_op jit(solution)/shard_map/all_gather | solution.py:298
  2820.4 1369.8 %all-reduce.3.cloned.1.call-start = ((), (), s32[]{:S(2)}) async-start(), calls=%async_computation.11 | async-start | bytes 18874368 | tf_op jit(solution)/shard_map/psum | solution.py:299
  3921.1 1.6 copy-start.11
  3921.1 1.6 copy-start.25
  3921.1 1.6 copy-start.36
  3921.1 1.6 copy-start.39
  3939.3 2.5 copy-start.41
  3939.3 2.5 copy-start.42
  3939.3 50.1 %copy-start.14 = (f32[256,2048]{1,0:T(8,128)S(1)}, f32[256,2048]{1,0:T(8,128)}, u32[]{:S(2)}) copy-start(f32[256,2048]{1,0:T(8,128)} %copy-done.12) | copy-start | bytes 6291460
  (7 other events, 6.6 us)
Sparse Core Ops, SparseCore 0:
  9.5 483.8 all-gather.11
  495.5 124.4 all-gather.13
  622.1 872.0 all-gather.15
  1495.6 441.0 all-gather.17
  2282.3 538.0 reduce-scatter.4
  2824.2 1084.4 reduce-scatter.6
  3910.2 107.1 all-gather.19
  4020.4 169.7 all-reduce.2
